TPU v7x, 32 devices: a whole 2x2x4 slice. The times are simulated.
32 devices in a mesh: ep: 8 (over z, y), dp: 4 (over x, core).
Axes of the slice: x: 2, y: 2, z: 4, core: 2. Of those that a mesh axis runs over, the one named last changes fastest.
Arguments:
- row_inputs: bfloat16 [4, 1024, 2048], P('dp', 'ep'), may hold values from -6 to 6
- hidden_grad: bfloat16 [4, 1024, 384], P('dp', 'ep'), may hold values from -6 to 6
- router_weight: bfloat16 [4, 1024], P('dp', 'ep'), may hold values from 0.049804688 to 1
- row_counts: int32 [4, 8, 2], P('dp', 'ep'), may hold values from 0 to 128, as said below
- row_owner: int32 [4, 1024, 1], P('dp', 'ep'), may hold values from 0 to 7; in each aligned block of 128 rows (0 to 127, 128 to 255, ..., all dimensions but the last counted through in order) at most 24 rows name the same one
- row_position: int32 [4, 1024], P('dp', 'ep'), may hold values from 0 to 127
- replica_expert: int32 [8], replicated, may hold values from 0 to 7, each once
- gate_up: bfloat16 [8, 2048, 768], P('ep', 'dp'), may hold values from -0.125 to 0.125
Outputs:
- token_grad: bfloat16 [4, 1024, 2048], P('dp', 'ep')
- weight_grad: float32 [8, 2048, 768], P('ep', 'dp')
Inputs may be any that keep to these rules, and one draw needn't show every extreme that they name: `row_counts`: for each data index and ep index: live rows of the home slot, then of the replica slot; together at most 128, and exactly 128 on some device of every data index. `row_owner`: within the rows of one device at most 24 rows name the same owner; some device has exactly 24 rows naming one owner. `replica_expert`: A permutation: every expert has exactly one replica slot.
All inputs are finite; a program needn't handle non-finite values.
Results may differ from a plain program's by a relative error of at most 0.012.
Values may be sent and summed in bfloat16 or wider, within the bound.
No kernel may reach another device: no remote copies, remote signals or barrier semaphores. Data moves between devices by JAX's collectives and lax.ppermute only.
A program may use at most 64 MiB of HBM per device.

v0:
```python
import jax
import jax.numpy as jnp
from jax import lax
from jax.sharding import PartitionSpec as P

D = 2048
HIDDEN_SIZE = 384
ROWS = 128
TOK_DEV = 128


def slot_terms(own_rows, own_grads, own_probs, live_rows, weights):
    pre = jnp.dot(own_rows, weights, preferred_element_type=jnp.float32)
    gate_pre = pre[:, :HIDDEN_SIZE]
    up_pre = pre[:, HIDDEN_SIZE:]
    sigmoid_gate = jax.nn.sigmoid(gate_pre)
    act_grad = jnp.where(
        live_rows[:, None],
        own_probs.astype(jnp.float32)[:, None] * own_grads.astype(jnp.float32),
        jnp.float32(0.0),
    )
    up_grad = act_grad * gate_pre * sigmoid_gate
    gate_grad = act_grad * up_pre * sigmoid_gate * (1.0 + gate_pre * (1.0 - sigmoid_gate))
    pre_grad = jnp.concatenate([gate_grad, up_grad], 1).astype(jnp.bfloat16)
    row_grad = lax.dot_general(
        pre_grad, weights, (((1,), (1,)), ((), ())), preferred_element_type=jnp.float32
    )
    weight_part = lax.dot_general(
        own_rows, pre_grad, (((0,), (0,)), ((), ())), preferred_element_type=jnp.float32
    )
    return (row_grad, weight_part.astype(jnp.bfloat16))


def body(
    row_inputs,
    hidden_grad,
    router_weight,
    row_counts,
    row_owner,
    row_position,
    replica_expert,
    gate_up,
):
    devices = lax.axis_size("ep")
    own_rows = row_inputs[0]
    own_grads = hidden_grad[0]
    own_probs = router_weight[0]
    positions = jnp.arange(ROWS, dtype=jnp.int32)
    home_count = row_counts[0, 0, 0]
    home_live = positions < home_count
    rep_live = (positions >= home_count) & (positions < home_count + row_counts[0, 0, 1])
    target = row_owner[0, :, 0] * TOK_DEV + row_position[0]
    home_shard = gate_up[0]
    inverse = (
        jnp.zeros((devices,), jnp.int32)
        .at[replica_expert]
        .set(jnp.arange(devices, dtype=jnp.int32))
    )
    row_tags = jnp.where(rep_live, target, -1)
    spread = (
        lax.all_to_all(
            own_rows.reshape(devices, -1, D), "ep", split_axis=0, concat_axis=0, tiled=True
        ),
        lax.all_to_all(
            own_grads.reshape(devices, -1, HIDDEN_SIZE),
            "ep",
            split_axis=0,
            concat_axis=0,
            tiled=True,
        ),
        lax.all_to_all(
            own_probs.reshape(devices, -1), "ep", split_axis=0, concat_axis=0, tiled=True
        ),
        lax.all_to_all(
            row_tags.reshape(devices, -1), "ep", split_axis=0, concat_axis=0, tiled=True
        ),
    )
    routed_rows = jnp.take(spread[0], inverse, axis=0)
    routed_grads = jnp.take(spread[1], inverse, axis=0)
    routed_probs = jnp.take(spread[2], inverse, axis=0)
    routed_tags = jnp.take(spread[3], inverse, axis=0)
    arrived = (
        lax.all_to_all(routed_rows, "ep", split_axis=0, concat_axis=0, tiled=True),
        lax.all_to_all(routed_grads, "ep", split_axis=0, concat_axis=0, tiled=True),
        lax.all_to_all(routed_probs, "ep", split_axis=0, concat_axis=0, tiled=True),
        lax.all_to_all(routed_tags, "ep", split_axis=0, concat_axis=0, tiled=True),
    )
    far_tags = arrived[3].reshape(ROWS)
    full_weights = lax.all_gather(home_shard, "dp", axis=0, tiled=True)
    home_dx, home_part = slot_terms(own_rows, own_grads, own_probs, home_live, full_weights)
    rep_dx, rep_part = slot_terms(
        arrived[0].reshape(ROWS, D),
        arrived[1].reshape(ROWS, HIDDEN_SIZE),
        arrived[2].reshape(ROWS),
        far_tags >= 0,
        full_weights,
    )
    summed = home_part.astype(jnp.float32) + rep_part.astype(jnp.float32)
    row_dx = jnp.concatenate([home_dx, rep_dx], 0).astype(jnp.bfloat16)
    row_target = jnp.concatenate([jnp.where(home_live, target, -1), far_tags], 0)
    capacity = max(2, 3 * ROWS // (2 * devices)) * (row_dx.shape[0] // ROWS)
    live_target = row_target >= 0
    dest_device = jnp.where(live_target, row_target // TOK_DEV, devices)
    onehot = (dest_device[:, None] == jnp.arange(devices, dtype=jnp.int32)[None, :]).astype(
        jnp.int32
    )
    row_rank = jnp.sum(jnp.cumsum(onehot, 0) * onehot, 1) - 1
    place_index = jnp.where(live_target, dest_device * capacity + row_rank, devices * capacity)
    buffer = (
        jnp.zeros((devices * capacity, D), jnp.bfloat16).at[place_index].set(row_dx, mode="drop")
    )
    token_slots = (
        jnp.full((devices * capacity,), -1, jnp.int32)
        .at[place_index]
        .set(row_target % TOK_DEV, mode="drop")
    )
    received, where_to = (
        lax.all_to_all(
            buffer.reshape(devices, capacity, D), "ep", split_axis=0, concat_axis=0, tiled=True
        ),
        lax.all_to_all(
            token_slots.reshape(devices, capacity), "ep", split_axis=0, concat_axis=0, tiled=True
        ),
    )
    token_onehot = (
        where_to.reshape(1, -1) == jnp.arange(TOK_DEV, dtype=jnp.int32)[:, None]
    ).astype(jnp.bfloat16)
    token_grad = jnp.dot(
        token_onehot, received.reshape(-1, D), preferred_element_type=jnp.float32
    ).astype(jnp.bfloat16)
    weight_grad = lax.psum_scatter(
        summed.astype(jnp.bfloat16), "dp", scatter_dimension=0, tiled=True
    ).astype(jnp.float32)
    return (token_grad[None], weight_grad[None])


def solution(mesh):
    placed = (
        P("dp", "ep", None),
        P("dp", "ep", None),
        P("dp", "ep"),
        P("dp", "ep", None),
        P("dp", "ep", None),
        P("dp", "ep"),
        P(),
        P("ep", "dp", None),
    )
    return jax.shard_map(
        body,
        mesh=mesh,
        in_specs=placed,
        out_specs=(P("dp", "ep", None), P("ep", "dp", None)),
        check_vma=False,
    )
```

profile of v0, /device:TPU:0, one launch (start us, length us, event | category | flops | bytes accessed | tf_op | source)
XLA Modules:
  0.0 183.7 jit_solution(488554558450376705)
XLA Ops:
  10.4 7.3 %all-to-all-start.3 = ((bf16[8,1,16]{2,1,0:T(2,128)(2,1)}), bf16[8,1,16]{2,1,0:T(2,128)(2,1)S(1)}, u32[]{:S(2)}, u32[]{:S(2)}) async-start(bf16[8,1,16]{2,1,0:T(2,128)(2,1)} %all_to_all.57), calls=%async_computation.3 | async-start | bytes 8192 | tf_op jit(solution)/shard_map/all_to_all | solution.py:71
  25.7 6.0 %all-to-all-start = ((s32[8,1,16]{2,1,0:T(1,128)}), s32[8,1,16]{2,1,0:T(1,128)S(1)}, u32[]{:S(2)}, u32[]{:S(2)}) async-start(s32[8,1,16]{2,1,0:T(1,128)} %bitcast.5), calls=%async_computation | async-start | bytes 8192 | tf_op jit(solution)/shard_map/all_to_all | solution.py:74
  32.3 5.8 %all-to-all-done = s32[8,1,16]{2,1,0:T(1,128)S(1)} async-done(((s32[8,1,16]{2,1,0:T(1,128)}), s32[8,1,16]{2,1,0:T(1,128)S(1)}, u32[]{:S(2)}, u32[]{:S(2)}) %all-to-all-start) | async-done | bytes 544 | tf_op jit(solution)/shard_map/all_to_all | solution.py:74
  38.1 8.8 %all_to_all.68 = bf16[8,1,16]{2,1,0:T(2,128)(2,1)S(1)} all-to-all(bf16[8,1,16]{2,1,0:T(2,128)(2,1)S(1)} %copy.23), channel_id=1, replica_groups=mesh['ep'=8,'dp'=4] {'ep'}, dimensions={0} | all-to-all | bytes 512 | tf_op jit(solution)/shard_map/all_to_all | solution.py:85
  46.9 3.5 %all-to-all-start.7 = ((bf16[8,16,2048]{2,1,0:T(8,128)(2,1)}), bf16[8,16,2048]{2,1,0:T(8,128)(2,1)S(1)}, u32[]{:S(2)}, u32[]{:S(2)}) async-start(bf16[8,16,2048]{2,1,0:T(8,128)(2,1)} %bitcast.84), calls=%async_computation.7 | async-start | bytes 1048576 | tf_op jit(solution)/shard_map/all_to_all | solution.py:61
  51.7 10.3 %all-to-all-done.7 = bf16[8,16,2048]{2,1,0:T(8,128)(2,1)S(1)} async-done(((bf16[8,16,2048]{2,1,0:T(8,128)(2,1)}), bf16[8,16,2048]{2,1,0:T(8,128)(2,1)S(1)}, u32[]{:S(2)}, u32[]{:S(2)}) %all-to-all-start.7) | async-done | bytes 524320 | tf_op jit(solution)/shard_map/all_to_all | solution.py:61
  62.0 3.7 %all-to-all-start.1 = ((s32[8,1,16]{2,1,0:T(1,128)}), s32[8,1,16]{2,1,0:T(1,128)S(1)}, u32[]{:S(2)}, u32[]{:S(2)}) async-start(s32[8,1,16]{2,1,0:T(1,128)} %bitcast.8), calls=%async_computation.1 | async-start | bytes 8192 | tf_op jit(solution)/shard_map/all_to_all | solution.py:86
  66.2 5.8 %all-to-all-done.1 = s32[8,1,16]{2,1,0:T(1,128)S(1)} async-done(((s32[8,1,16]{2,1,0:T(1,128)}), s32[8,1,16]{2,1,0:T(1,128)S(1)}, u32[]{:S(2)}, u32[]{:S(2)}) %all-to-all-start.1) | async-done | bytes 544 | tf_op jit(solution)/shard_map/all_to_all | solution.py:86
  72.1 3.4 %all-to-all-start.5 = ((bf16[8,16,384]{2,1,0:T(8,128)(2,1)}), bf16[8,16,384]{2,1,0:T(8,128)(2,1)S(1)}, u32[]{:S(2)}, u32[]{:S(2)}) async-start(bf16[8,16,384]{2,1,0:T(8,128)(2,1)} %bitcast.85), calls=%async_computation.5 | async-start | bytes 196608 | tf_op jit(solution)/shard_map/all_to_all | solution.py:64
  76.3 6.2 %all-to-all-done.5 = bf16[8,16,384]{2,1,0:T(8,128)(2,1)S(1)} async-done(((bf16[8,16,384]{2,1,0:T(8,128)(2,1)}), bf16[8,16,384]{2,1,0:T(8,128)(2,1)S(1)}, u32[]{:S(2)}, u32[]{:S(2)}) %all-to-all-start.5) | async-done | bytes 98336 | tf_op jit(solution)/shard_map/all_to_all | solution.py:64
  82.5 3.5 %all-to-all-start.8 = ((bf16[8,16,2048]{2,1,0:T(8,128)(2,1)}), bf16[8,16,2048]{2,1,0:T(8,128)(2,1)S(1)}, u32[]{:S(2)}, u32[]{:S(2)}) async-start(bf16[8,16,2048]{2,1,0:T(8,128)(2,1)} %broadcast_select_fusion), calls=%async_computation.8 | async-start | bytes 1048576 | tf_op jit(solution)/shard_map/all_to_all | solution.py:83
  88.1 8.8 %all-to-all-done.8 = bf16[8,16,2048]{2,1,0:T(8,128)(2,1)S(1)} async-done(((bf16[8,16,2048]{2,1,0:T(8,128)(2,1)}), bf16[8,16,2048]{2,1,0:T(8,128)(2,1)S(1)}, u32[]{:S(2)}, u32[]{:S(2)}) %all-to-all-start.8) | async-done | bytes 524320 | tf_op jit(solution)/shard_map/all_to_all | solution.py:83
  96.9 3.7 %all-to-all-start.6 = ((bf16[8,16,384]{2,1,0:T(8,128)(2,1)}), bf16[8,16,384]{2,1,0:T(8,128)(2,1)S(1)}, u32[]{:S(2)}, u32[]{:S(2)}) async-start(bf16[8,16,384]{2,1,0:T(8,128)(2,1)} %broadcast_select_fusion.1), calls=%async_computation.6 | async-start | bytes 196608 | tf_op jit(solution)/shard_map/all_to_all | solution.py:84
  100.7 2.5 %fusion.3 = f32[128,768]{1,0:T(8,128)S(1)} fusion(bf16[128,2048]{1,0:T(8,128)(2,1)S(1)} %bitcast.81, bf16[1,2048,768]{2,1,0:T(8,128)(2,1)} %all-gather.3.cloned.1.call-done), kind=kOutput, calls=%fused_computation.13 | convolution fusion | flops 402653184 | bytes 4063232 | tf_op jit(solution)/shard_map/dot_general | solution.py:13
  103.2 4.6 %all-to-all-done.6 = bf16[8,16,384]{2,1,0:T(8,128)(2,1)S(1)} async-done(((bf16[8,16,384]{2,1,0:T(8,128)(2,1)}), bf16[8,16,384]{2,1,0:T(8,128)(2,1)S(1)}, u32[]{:S(2)}, u32[]{:S(2)}) %all-to-all-start.6) | async-done | bytes 98336 | tf_op jit(solution)/shard_map/all_to_all | solution.py:84
  108.0 2.2 %convolution_convert_fusion = bf16[2048,768]{0,1:T(8,128)(2,1)S(1)} fusion(bf16[128,2048]{1,0:T(8,128)(2,1)} %bitcast.82, bf16[128,384]{1,0:T(8,128)(2,1)S(1)} %get-tuple-element.13, bf16[128,384]{1,0:T(8,128)(2,1)S(1)} %get-tuple-element.12), kind=kOutput, calls=%fused_computation.9 | convolution fusion | flops 404619264 | bytes 3866624 | tf_op jit(solution)/shard_map/dot_general | solution.py:28
  111.2 2.7 %fusion = bf16[2048,768]{0,1:T(8,128)(2,1)} fusion(bf16[2048,768]{0,1:T(8,128)(2,1)S(1)} %convolution_convert_fusion, bf16[1,128,2048]{2,1,0:T(8,128)(2,1)S(1)} %copy-done.2, bf16[128,384]{1,0:T(8,128)(2,1)S(1)} %get-tuple-element.11, bf16[128,384]{1,0:T(8,128)(2,1)S(1)} %get-tuple-element.10), kind=kOutput, calls=%fused_computation.8 | convolution fusion | flops 410910720 | bytes 7012352 | tf_op jit(solution)/shard_map/dot_general | solution.py:28
  122.1 3.3 %all-to-all-start.2 = ((s32[8,1,48]{2,1,0:T(1,128)}), s32[8,1,48]{2,1,0:T(1,128)S(1)}, u32[]{:S(2)}, u32[]{:S(2)}) async-start(s32[8,1,48]{2,1,0:T(1,128)} %all_to_all.46), calls=%async_computation.2 | async-start | bytes 8192 | tf_op jit(solution)/shard_map/all_to_all | solution.py:121
  125.4 1.9 %fusion.12 = bf16[128,2048]{1,0:T(8,128)(2,1)} fusion(bf16[1,2048,768]{2,1,0:T(8,128)(2,1)S(1)} %copy-done, bf16[128,384]{1,0:T(8,128)(2,1)S(1)} %get-tuple-element.13, bf16[128,384]{1,0:T(8,128)(2,1)S(1)} %get-tuple-element.12), kind=kOutput, calls=%fused_computation.20 | convolution fusion | flops 403308544 | bytes 3866624 | tf_op jit(solution)/shard_map/dot_general | solution.py:25
  127.3 1.9 %fusion.9 = bf16[128,2048]{1,0:T(8,128)(2,1)} fusion(bf16[1,2048,768]{2,1,0:T(8,128)(2,1)S(1)} %copy-done, bf16[128,384]{1,0:T(8,128)(2,1)S(1)} %get-tuple-element.11, bf16[128,384]{1,0:T(8,128)(2,1)S(1)} %get-tuple-element.10), kind=kOutput, calls=%fused_computation.19 | convolution fusion | flops 403308544 | bytes 3866624 | tf_op jit(solution)/shard_map/dot_general | solution.py:25
  129.2 4.1 %scatter_custom_fusion.2 = bf16[384,2048]{1,0:T(8,128)(2,1)} fusion(s32[256]{0:T(256)S(1)} %bitcast.93, bf16[128,2048]{1,0:T(8,128)(2,1)} %fusion.12, bf16[]{:T(256)} %constant.134, bf16[128,2048]{1,0:T(8,128)(2,1)} %fusion.9, bf16[]{:T(256)} %constant.108.clone.1), kind=kCustom, calls=%fused_computation.23 | custom fusion | flops 2097152 | bytes 2621444 | tf_op jit(solution)/shard_map/scatter | solution.py:110
  133.3 5.9 %all-to-all-start.9 = ((bf16[8,48,2048]{2,1,0:T(8,128)(2,1)}), bf16[8,48,2048]{2,1,0:T(8,128)(2,1)S(1)}, u32[]{:S(2)}, u32[]{:S(2)}) async-start(bf16[8,48,2048]{2,1,0:T(8,128)(2,1)} %bitcast.25), calls=%async_computation.9 | async-start | bytes 3145728 | tf_op jit(solution)/shard_map/all_to_all | solution.py:118
  140.1 32.6 %all-to-all-done.9 = bf16[8,48,2048]{2,1,0:T(8,128)(2,1)S(1)} async-done(((bf16[8,48,2048]{2,1,0:T(8,128)(2,1)}), bf16[8,48,2048]{2,1,0:T(8,128)(2,1)S(1)}, u32[]{:S(2)}, u32[]{:S(2)}) %all-to-all-start.9) | async-done | bytes 1572896 | tf_op jit(solution)/shard_map/all_to_all | solution.py:118
  175.3 1.6 copy.25
  (79 shorter events, 28.1 us)
Async XLA Ops:
  7.2 93.5 %all-gather.3.cloned.1.call-start = ((), (), s32[]{:S(2)}) async-start(), calls=%async_computation.12 | async-start | bytes 3932160 | tf_op jit(solution)/shard_map/all_gather | solution.py:89
  10.4 15.2 %all-to-all-start.3 = ((bf16[8,1,16]{2,1,0:T(2,128)(2,1)}), bf16[8,1,16]{2,1,0:T(2,128)(2,1)S(1)}, u32[]{:S(2)}, u32[]{:S(2)}) async-start(bf16[8,1,16]{2,1,0:T(2,128)(2,1)} %all_to_all.57), calls=%async_computation.3 | async-start | bytes 8192 | tf_op jit(solution)/shard_map/all_to_all | solution.py:71
  25.7 12.4 %all-to-all-start = ((s32[8,1,16]{2,1,0:T(1,128)}), s32[8,1,16]{2,1,0:T(1,128)S(1)}, u32[]{:S(2)}, u32[]{:S(2)}) async-start(s32[8,1,16]{2,1,0:T(1,128)} %bitcast.5), calls=%async_computation | async-start | bytes 8192 | tf_op jit(solution)/shard_map/all_to_all | solution.py:74
  46.9 15.0 %all-to-all-start.7 = ((bf16[8,16,2048]{2,1,0:T(8,128)(2,1)}), bf16[8,16,2048]{2,1,0:T(8,128)(2,1)S(1)}, u32[]{:S(2)}, u32[]{:S(2)}) async-start(bf16[8,16,2048]{2,1,0:T(8,128)(2,1)} %bitcast.84), calls=%async_computation.7 | async-start | bytes 1048576 | tf_op jit(solution)/shard_map/all_to_all | solution.py:61
  62.0 10.1 %all-to-all-start.1 = ((s32[8,1,16]{2,1,0:T(1,128)}), s32[8,1,16]{2,1,0:T(1,128)S(1)}, u32[]{:S(2)}, u32[]{:S(2)}) async-start(s32[8,1,16]{2,1,0:T(1,128)} %bitcast.8), calls=%async_computation.1 | async-start | bytes 8192 | tf_op jit(solution)/shard_map/all_to_all | solution.py:86
  72.1 10.4 %all-to-all-start.5 = ((bf16[8,16,384]{2,1,0:T(8,128)(2,1)}), bf16[8,16,384]{2,1,0:T(8,128)(2,1)S(1)}, u32[]{:S(2)}, u32[]{:S(2)}) async-start(bf16[8,16,384]{2,1,0:T(8,128)(2,1)} %bitcast.85), calls=%async_computation.5 | async-start | bytes 196608 | tf_op jit(solution)/shard_map/all_to_all | solution.py:64
  82.5 14.4 %all-to-all-start.8 = ((bf16[8,16,2048]{2,1,0:T(8,128)(2,1)}), bf16[8,16,2048]{2,1,0:T(8,128)(2,1)S(1)}, u32[]{:S(2)}, u32[]{:S(2)}) async-start(bf16[8,16,2048]{2,1,0:T(8,128)(2,1)} %broadcast_select_fusion), calls=%async_computation.8 | async-start | bytes 1048576 | tf_op jit(solution)/shard_map/all_to_all | solution.py:83
  86.8 21.1 %copy-start.5 = (s32[128]{0:T(128)}, s32[128]{0:T(128)S(1)}, u32[]{:S(2)}) copy-start(s32[128]{0:T(128)S(1)} %concatenate.72) | copy-start | bytes 1540
  96.9 11.0 %copy-start.1 = (bf16[8,16,2048]{2,1,0:T(8,128)(2,1)}, bf16[8,16,2048]{2,1,0:T(8,128)(2,1)S(1)}, u32[]{:S(2)}) copy-start(bf16[8,16,2048]{2,1,0:T(8,128)(2,1)S(1)} %all-to-all-done.8) | copy-start | bytes 1572868
  96.9 10.8 %all-to-all-start.6 = ((bf16[8,16,384]{2,1,0:T(8,128)(2,1)}), bf16[8,16,384]{2,1,0:T(8,128)(2,1)S(1)}, u32[]{:S(2)}, u32[]{:S(2)}) async-start(bf16[8,16,384]{2,1,0:T(8,128)(2,1)} %broadcast_select_fusion.1), calls=%async_computation.6 | async-start | bytes 196608 | tf_op jit(solution)/shard_map/all_to_all | solution.py:84
  100.6 73.3 %reduce-scatter.2.cloned.1.call-start = ((), (), s32[]{:S(2)}) async-start(), calls=%async_computation.11 | async-start | bytes 3932160 | tf_op jit(solution)/shard_map/reduce_scatter | solution.py:131
  107.9 2.2 %copy-start = (bf16[1,2048,768]{2,1,0:T(8,128)(2,1)S(1)}, bf16[1,2048,768]{2,1,0:T(8,128)(2,1)}, u32[]{:S(2)}) copy-start(bf16[1,2048,768]{2,1,0:T(8,128)(2,1)} %all-gather.3.cloned.1.call-done) | copy-start | bytes 9437188
  107.9 2.2 %copy-start.2 = (bf16[1,128,2048]{2,1,0:T(8,128)(2,1)S(1)}, bf16[1,128,2048]{2,1,0:T(8,128)(2,1)}, u32[]{:S(2)}) copy-start(bf16[1,128,2048]{2,1,0:T(8,128)(2,1)} %param.8) | copy-start | bytes 1572868
  110.2 0.9 copy-start.3
  113.9 0.7 copy-start.6
  113.9 0.7 copy-start.7
  117.2 0.5 copy-start.4
  122.1 11.2 %all-to-all-start.2 = ((s32[8,1,48]{2,1,0:T(1,128)}), s32[8,1,48]{2,1,0:T(1,128)S(1)}, u32[]{:S(2)}, u32[]{:S(2)}) async-start(s32[8,1,48]{2,1,0:T(1,128)} %all_to_all.46), calls=%async_computation.2 | async-start | bytes 8192 | tf_op jit(solution)/shard_map/all_to_all | solution.py:121
  133.3 39.3 %all-to-all-start.9 = ((bf16[8,48,2048]{2,1,0:T(8,128)(2,1)}), bf16[8,48,2048]{2,1,0:T(8,128)(2,1)S(1)}, u32[]{:S(2)}, u32[]{:S(2)}) async-start(bf16[8,48,2048]{2,1,0:T(8,128)(2,1)} %bitcast.25), calls=%async_computation.9 | async-start | bytes 3145728 | tf_op jit(solution)/shard_map/all_to_all | solution.py:118
Sparse Core Ops, SparseCore 0:
  9.5 31.2 all-gather.2
  114.1 35.3 reduce-scatter.1
where the time goes:
time: 185 us; the launch traced here: 184 us
  waiting for transfers between devices  74.8 us (40%)
  starting transfers between devices  40.3 us (22%)
  other arithmetic  19.4 us (10%)
  between operations  15.6 us (8%)
  matrix products  13.1 us (7%)
  local copies, waits for them, and re-layouts  11.8 us (6%)
  blocking collectives  8.85 us (5%)
    all_to_all x1, waiting for transfers between devices, body(): lax.all_to_all(buffer.reshape(devices, capacity, D), 'ep', split_axis=0,...  32.6 us
    all_to_all x1, waiting for transfers between devices, body(): lax.all_to_all(own_rows.reshape(devices, -1, D), 'ep', split_axis=0, conc...  10.3 us
    all_to_all x1, blocking collectives, body(): lax.all_to_all(routed_probs, 'ep', split_axis=0, concat_axis=0, tiled=True)  8.85 us
    all_to_all x1, waiting for transfers between devices, body(): lax.all_to_all(routed_rows, 'ep', split_axis=0, concat_axis=0, tiled=True)  8.79 us
    all_to_all x1, starting transfers between devices, body(): lax.all_to_all(own_probs.reshape(devices, -1), 'ep', split_axis=0, concat...  7.31 us
    all_to_all x1, waiting for transfers between devices, body(): lax.all_to_all(own_grads.reshape(devices, -1, HIDDEN_SIZE), 'ep', split_a...  6.15 us
    all_to_all x1, starting transfers between devices, body(): lax.all_to_all(row_tags.reshape(devices, -1), 'ep', split_axis=0, concat_...  6.01 us
    all_to_all x1, starting transfers between devices, body(): lax.all_to_all(buffer.reshape(devices, capacity, D), 'ep', split_axis=0,...  5.93 us
  transfers between devices with their start and end apart: 11, of which 7 were waited for; matrix products, arithmetic and copies ran while one was open for 18% of the time, Pallas kernels for 0%

commit v1 on v0

v1 whole, which is shorter than its diff:
```python
import functools

import jax
import jax.numpy as jnp
from jax import lax
from jax.experimental import pallas as pl
from jax.experimental.pallas import tpu as pltpu
from jax.sharding import PartitionSpec as P

F32 = jnp.float32
BF16 = jnp.bfloat16
VMEM = pl.BlockSpec(memory_space=pltpu.VMEM)
SMEM = pl.BlockSpec(memory_space=pltpu.SMEM)


def dot(a, b, dims=((1,), (0,))):
    return lax.dot_general(a, b, (dims, ((), ())), preferred_element_type=F32)


def routing_kernel(ids, rep_row, meta, ctl, where_home, where_rep, *, cap):
    n, rows = meta.shape[0], meta.shape[1] // 2
    me, source = ids[0], ids[1]
    total = n * rows
    r0 = lax.broadcasted_iota(jnp.int32, (rows, rows), 0)
    r1 = lax.broadcasted_iota(jnp.int32, (rows, rows), 1)
    before = (r0 < r1).astype(BF16)

    def parts(code):
        rep = code >= total
        live_target = jnp.where(rep, code - total, code)
        owner = jnp.where(code < 0, -1, lax.div(jnp.maximum(live_target, 0), rows))
        return owner, live_target - owner * rows, (code >= 0) & ~rep, rep

    code = meta[:, :rows].astype(jnp.int32)
    owner, position, home, rep = parts(code)
    lanes = lax.broadcasted_iota(jnp.int32, where_home.shape, 1)

    def positions_of(mask):
        rank = dot(mask.astype(BF16), before).astype(jnp.int32)
        found = jnp.zeros(where_home.shape, jnp.int32)
        for slot in range(cap):
            hit = jnp.where(mask & (rank == slot), position + 1, 0)
            found = jnp.where(lanes == slot, jnp.sum(hit, 1, keepdims=True), found)
        return found

    mine = owner == me
    where_home[...] = positions_of(mine & home) - 1
    e0 = lax.broadcasted_iota(jnp.int32, (n, n), 0)
    to_expert = (rep_row[...] == e0).astype(BF16)
    by_block = positions_of(mine & rep).astype(F32).astype(BF16)
    where_rep[...] = dot(to_expert, by_block).astype(jnp.int32) - 1

    owners = lax.broadcasted_iota(jnp.int32, (n, rows), 0)
    for which, block in ((0, me), (1, source)):
        line = meta[pl.ds(block, 1), :]
        own, _, h, r = parts(line[:, :rows].astype(jnp.int32))
        live = r if which else h
        held = (owners == own) & live
        count = dot(held.astype(BF16), before)
        rank = jnp.sum(jnp.where(held, count, 0.0), 0, keepdims=True)
        slot = jnp.where(live, own.astype(F32) * cap + rank, -1.0)
        ctl[2 * which : 2 * which + 1, :] = slot
        ctl[2 * which + 1 : 2 * which + 2, :] = jnp.where(live, line[:, rows:], 0.0)


def expert_kernel(ids, data, ctl, *refs, which, pieces, width, hidden):
    weights, (send, grads) = refs[:pieces], refs[pieces:]
    d = ids[2]
    rows = data.shape[0]
    cols = [pl.ds(pl.multiple_of((d ^ m) * width, width), width) for m in range(pieces)]
    pre = dot(data[:, cols[0]], weights[0][...])
    for m in range(1, pieces):
        pre = pre + dot(data[:, cols[m]], weights[m][...])
    r0 = lax.broadcasted_iota(jnp.int32, (rows, rows), 0)
    r1 = lax.broadcasted_iota(jnp.int32, (rows, rows), 1)
    prob = jnp.sum(
        jnp.where(r0 == r1, ctl[2 * which + 1 : 2 * which + 2, :], 0.0), 1, keepdims=True
    )
    act_grad = prob * data[:, pieces * width :].astype(F32)
    gate, up = pre[:, :hidden], pre[:, hidden:]
    s = jax.nn.sigmoid(gate)
    gate_grad = act_grad * up * s * (1.0 + gate * (1.0 - s))
    up_grad = act_grad * gate * s
    pre_grad = jnp.concatenate([gate_grad, up_grad], 1).astype(BF16)
    grads[...] = pre_grad
    slots = lax.broadcasted_iota(jnp.int32, (send.shape[0], rows), 0)
    place = (slots == ctl[2 * which : 2 * which + 1, :].astype(jnp.int32)).astype(BF16)
    placed = dot(place, pre_grad).astype(BF16)
    for m in range(pieces):
        send[:, cols[m]] = dot(placed, weights[m][...], ((1,), (1,))).astype(BF16)


def weight_kernel(ids, home_data, rep_data, home_grads, rep_grads, keep, give, *, pieces, width):
    d = ids[2]
    grads = jnp.concatenate([home_grads[...], rep_grads[...]], 0)
    for m in range(pieces):
        cols = pl.ds(pl.multiple_of((d ^ m) * width, width), width)
        data = jnp.concatenate([home_data[:, cols], rep_data[:, cols]], 0)
        part = dot(data, grads, ((0,), (0,))).astype(BF16)
        (give if m & 1 else keep)[m >> 1] = part


def body(row_inputs, hidden_grad, router_weight, row_counts, row_owner, row_position, replica_expert, gate_up):
    n, nd = lax.axis_size("ep"), lax.axis_size("dp")
    me, d = lax.axis_index("ep"), lax.axis_index("dp")
    rows, model = row_inputs.shape[1:]
    hidden = hidden_grad.shape[2]
    width = gate_up.shape[1]
    cap = max(2, 3 * rows // (2 * n))
    params = pltpu.CompilerParams(vmem_limit_bytes=48 << 20)

    def swap(array, bit):
        return lax.ppermute(array, "dp", [(i, i ^ bit) for i in range(nd)])

    def exchange(array):
        return lax.all_to_all(array, "ep", split_axis=0, concat_axis=0, tiled=True)

    own = gate_up[0]
    pieces = {0: own}
    bit = nd >> 1
    while bit:
        for m in list(pieces):
            pieces[m | bit] = swap(pieces[m], bit)
        bit >>= 1
    weights = [pieces[m] for m in range(nd)]

    payload = jnp.concatenate([row_inputs[0], hidden_grad[0]], 1)
    experts = jnp.arange(n, dtype=jnp.int32)
    inverse = jnp.sum(jnp.where(replica_expert[None, :] == experts[:, None], experts[None, :], 0), 1)
    spread = exchange(payload.reshape(n, rows // n, -1))
    routed = jnp.take(spread, inverse, axis=0, mode="clip")
    arrived = exchange(routed).reshape(rows, -1)

    at = jnp.arange(rows, dtype=jnp.int32)
    first, second = row_counts[0, 0, 0], row_counts[0, 0, 1]
    target = row_owner[0, :, 0] * rows + row_position[0]
    code = jnp.where(at < first, target, jnp.where(at < first + second, target + n * rows, -1))
    meta = jnp.concatenate([code.astype(F32), router_weight[0].astype(F32)])
    meta = exchange(jnp.broadcast_to(meta[None, None, :], (n, 1, 2 * rows))).reshape(n, 2 * rows)

    ids = jnp.stack([me, jnp.sum(jnp.where(experts == me, inverse, 0)), d]).astype(jnp.int32)
    ctl, where_home, where_rep = pl.pallas_call(
        functools.partial(routing_kernel, cap=cap),
        out_shape=(
            jax.ShapeDtypeStruct((8, rows), F32),
            jax.ShapeDtypeStruct((n, cap), jnp.int32),
            jax.ShapeDtypeStruct((n, cap), jnp.int32),
        ),
        in_specs=[SMEM, VMEM, VMEM],
        out_specs=(VMEM, VMEM, VMEM),
        name="routing",
    )(ids, replica_expert[None, :], meta)

    def expert(which, data):
        return pl.pallas_call(
            functools.partial(expert_kernel, which=which, pieces=nd, width=width, hidden=hidden),
            out_shape=(
                jax.ShapeDtypeStruct((n * cap, model), BF16),
                jax.ShapeDtypeStruct((rows, 2 * hidden), BF16),
            ),
            in_specs=[SMEM] + [VMEM] * (2 + nd),
            out_specs=(VMEM, VMEM),
            compiler_params=params,
            cost_estimate=pl.CostEstimate(flops=6 * rows * model * 2 * hidden, bytes_accessed=6 << 20, transcendentals=0),
            name=("home", "replica")[which],
        )(ids, data, ctl, *weights)

    tokens = jnp.arange(rows, dtype=jnp.int32)[:, None]

    def gathered(send, where_to):
        got = exchange(send.reshape(n, cap, model)).reshape(n * cap, model)
        pick = (where_to.reshape(1, -1) == tokens).astype(BF16)
        return jnp.dot(pick, got, preferred_element_type=F32)

    home_send, home_grads = expert(0, payload)
    home_tokens = gathered(home_send, where_home)
    rep_send, rep_grads = expert(1, arrived)
    token_grad = (home_tokens + gathered(rep_send, where_rep)).astype(BF16)

    keep, give = pl.pallas_call(
        functools.partial(weight_kernel, pieces=nd, width=width),
        out_shape=(jax.ShapeDtypeStruct((nd // 2, width, 2 * hidden), BF16),) * 2,
        in_specs=[SMEM] + [VMEM] * 4,
        out_specs=(VMEM, VMEM),
        compiler_params=params,
        cost_estimate=pl.CostEstimate(flops=8 * rows * model * hidden, bytes_accessed=6 << 20, transcendentals=0),
        name="weight_grad",
    )(ids, payload, arrived, home_grads, rep_grads)
    near = swap(give, 1)
    total = keep.astype(F32) + near.astype(F32)
    bit, held = nd >> 1, total
    while bit > 1:
        half = held.shape[0] // 2
        held = held[:half] + swap(held[half:].astype(BF16), bit).astype(F32)
        bit >>= 1
    return (token_grad[None], held)


def solution(mesh):
    placed = (
        P("dp", "ep", None),
        P("dp", "ep", None),
        P("dp", "ep"),
        P("dp", "ep", None),
        P("dp", "ep", None),
        P("dp", "ep"),
        P(),
        P("ep", "dp", None),
    )
    return jax.shard_map(
        body,
        mesh=mesh,
        in_specs=placed,
        out_specs=(P("dp", "ep", None), P("ep", "dp", None)),
        check_vma=False,
    )
```

time: 185 us -> 110 us (0.59)
  waiting for transfers between devices: 74.8 us -> 47.4 us
  starting transfers between devices: 40.3 us -> 26.6 us
  between operations: 15.6 us -> 2.12 us
  Pallas kernels: 0 us -> 13.1 us
  other arithmetic: 19.4 us -> 7.48 us
  blocking collectives: 8.85 us -> 0 us
  matrix products: 13.1 us -> 5.12 us
  local copies, waits for them, and re-layouts: 11.8 us -> 7.36 us
    all_to_all x9 -> x5, waiting for transfers between devices: 74.1 us -> 47.4 us  [exchange(): return lax.all_to_all(array, 'ep', split_axis=0, concat_axis=0, tiled=True)]
    all_to_all x9 -> x5, starting transfers between devices: 40.2 us -> 22.9 us  [exchange(): return lax.all_to_all(array, 'ep', split_axis=0, concat_axis=0, tiled=True)]
    pallas_call x0 -> x4, Pallas kernels: none -> 13.1 us  [the longest x2 8.67 us: expert(): pl.pallas_call(functools.partial(expert_kernel, which=which, pieces=nd, w...]
    all_to_all x1 -> x0, blocking collectives: 8.85 us -> none  [body(): lax.all_to_all(routed_probs, 'ep', split_axis=0, concat_axis=0, tiled=True)]
    dot_general x7 -> x2, matrix products: 13.1 us -> 5.12 us  [gathered(): return jnp.dot(pick, got, preferred_element_type=F32)]
    select_n x12 -> x0, other arithmetic: 7.47 us -> none  [the longest x2 1.78 us: body(): jnp.where(home_live, target, -1)]
    scatter x1 -> x0, other arithmetic: 4.11 us -> none  [body(): jnp.zeros((devices * capacity, D), jnp.bfloat16).at[place_index]]
    ppermute x0 -> x5, starting transfers between devices: none -> 3.61 us  [swap(): return lax.ppermute(array, 'dp', [(i, i ^ bit) for i in range(nd)])]
  transfers between devices with their start and end apart: 11 -> 10, of which waited for: 7 -> 5; matrix products, arithmetic and copies ran while one was open for 18% -> 11% of each run, Pallas kernels for 0% -> 12%
where the time goes in v1:
time: 110 us; the launch traced here: 109 us
  waiting for transfers between devices  47.4 us (43%)
  starting transfers between devices  26.6 us (24%)
  Pallas kernels  13.1 us (12%)
  other arithmetic  7.48 us (7%)
  local copies, waits for them, and re-layouts  7.36 us (7%)
  matrix products  5.12 us (5%)
  between operations  2.12 us (2%)
    all_to_all x5, waiting for transfers between devices, exchange(): return lax.all_to_all(array, 'ep', split_axis=0, concat_axis=0, tiled=True)  47.4 us
    all_to_all x5, starting transfers between devices, exchange(): return lax.all_to_all(array, 'ep', split_axis=0, concat_axis=0, tiled=True)  22.9 us
    pallas_call x2, Pallas kernels, expert(): pl.pallas_call(functools.partial(expert_kernel, which=which, pieces=nd, w...  8.67 us
    dot_general x2, matrix products, gathered(): return jnp.dot(pick, got, preferred_element_type=F32)  5.12 us
    unnamed x33, local copies, waits for them, and re-layouts  3.61 us
    ppermute x5, starting transfers between devices, swap(): return lax.ppermute(array, 'dp', [(i, i ^ bit) for i in range(nd)])  3.61 us
    pallas_call x1, Pallas kernels, body(): pl.pallas_call(functools.partial(weight_kernel, pieces=nd, width=width),...  2.7 us
    add x1, other arithmetic, body(): held = held[:half] + swap(held[half:].astype(BF16), bit).astype(F32)  2.42 us
  transfers between devices with their start and end apart: 10, of which 5 were waited for; matrix products, arithmetic and copies ran while one was open for 11% of the time, Pallas kernels for 12%

profile of v1, /device:TPU:0, one launch (start us, length us, event | category | flops | bytes accessed | tf_op | source)
XLA Modules:
  0.0 109.1 jit_solution(4752384609224254895)
XLA Ops:
  0.7 2.0 %pad_maximum_fusion.1 = bf16[8,16,2432]{2,1,0:T(8,128)(2,1)} fusion(bf16[8,16,384]{2,1,0:T(8,128)(2,1)} %bitcast.42, bf16[8,16,2048]{2,1,0:T(8,128)(2,1)} %bitcast.40), kind=kLoop, calls=%fused_computation.8 | loop fusion | flops 1245184 | bytes 1245184 | tf_op jit(solution)/shard_map/concatenate | solution.py:127
  2.7 7.3 %all-to-all-start.2 = ((bf16[8,16,2432]{2,1,0:T(8,128)(2,1)}), bf16[8,16,2432]{2,1,0:T(8,128)(2,1)S(1)}, u32[]{:S(2)}, u32[]{:S(2)}) async-start(bf16[8,16,2432]{2,1,0:T(8,128)(2,1)} %pad_maximum_fusion.1), calls=%async_computation.2 | async-start | bytes 1245184 | tf_op jit(solution)/shard_map/all_to_all | solution.py:116
  10.1 1.6 %collective-permute-start.1 = (bf16[512,768]{1,0:T(8,128)(2,1)S(1)}, bf16[512,768]{1,0:T(8,128)(2,1)S(1)}, u32[]{:S(2)}, u32[]{:S(2)}) collective-permute-start(bf16[512,768]{1,0:T(8,128)(2,1)S(1)} %bitcast.36), channel_id=1, source_target_pairs={{0,2},{1,3},{2,0},{3,1},{4,6},{5,7},{6,4},{7,5},{8,10},{9,11},{10,... | collective-permute-start | bytes 2359304 | tf_op jit(solution)/shard_map/ppermute | solution.py:113
  14.3 12.4 %all-to-all-done.2 = bf16[8,16,2432]{2,1,0:T(8,128)(2,1)S(1)} async-done(((bf16[8,16,2432]{2,1,0:T(8,128)(2,1)}), bf16[8,16,2432]{2,1,0:T(8,128)(2,1)S(1)}, u32[]{:S(2)}, u32[]{:S(2)}) %all-to-all-start.2) | async-done | bytes 622624 | tf_op jit(solution)/shard_map/all_to_all | solution.py:116
  27.2 3.6 %all-to-all-start = ((f32[8,1,256]{2,1,0:T(1,128)}), f32[8,1,256]{2,1,0:T(1,128)S(1)}, u32[]{:S(2)}, u32[]{:S(2)}) async-start(f32[8,1,256]{2,1,0:T(1,128)} %broadcast_in_dim.45), calls=%async_computation | async-start | bytes 16384 | tf_op jit(solution)/shard_map/all_to_all | solution.py:116
  30.9 1.4 %gather_fusion = bf16[8,16,2432]{2,1,0:T(8,128)(2,1)} fusion(bf16[8,16,2432]{2,1,0:T(8,128)(2,1)S(1)} %all-to-all-done.2, s32[1024]{0:T(1024)S(1)} %pad_clamp_fusion), kind=kCustom, calls=%fused_computation | custom fusion | bytes 1245216 | tf_op jit(solution)/shard_map/jit(_take)/gather | solution.py:131
  32.3 5.1 %all-to-all-done = f32[8,1,256]{2,1,0:T(1,128)S(1)} async-done(((f32[8,1,256]{2,1,0:T(1,128)}), f32[8,1,256]{2,1,0:T(1,128)S(1)}, u32[]{:S(2)}, u32[]{:S(2)}) %all-to-all-start) | async-done | bytes 8224 | tf_op jit(solution)/shard_map/all_to_all | solution.py:116
  37.4 3.5 %all-to-all-start.3 = ((bf16[8,16,2432]{2,1,0:T(8,128)(2,1)}), bf16[8,16,2432]{2,1,0:T(8,128)(2,1)S(1)}, u32[]{:S(2)}, u32[]{:S(2)}) async-start(bf16[8,16,2432]{2,1,0:T(8,128)(2,1)} %gather_fusion), calls=%async_computation.3 | async-start | bytes 1245184 | tf_op jit(solution)/shard_map/all_to_all | solution.py:116
  42.2 1.3 %pad_add_fusion.ids = s32[3]{0:T(128)} fusion(s32[1]{0:T(128)} %bitcast.2, s32[1]{0:T(128)} %bitcast.1, s32[1]{0:T(128)} %bitcast), kind=kLoop, calls=%fused_computation.24 | loop fusion | flops 6 | bytes 24 | tf_op jit(solution)/shard_map/stack | solution.py:141
  44.1 1.7 %routing.1 = (f32[8,128]{1,0:T(8,128)}, s32[8,24]{1,0:T(8,128)}, s32[8,24]{1,0:T(8,128)}) custom-call(s32[3]{0:T(128)} %pad_add_fusion.ids, s32[1,8]{1,0:T(1,128)} %bitcast.45, f32[8,256]{1,0:T(8,128)} %bitcast.44), custom_call_target="tpu_custom_call" | custom-call | tf_op jit(solution)/shard_map/routing/pallas_call | solution.py:142
  47.2 4.3 %home.1 = (bf16[192,2048]{1,0:T(8,128)(2,1)}, bf16[128,768]{1,0:T(8,128)(2,1)S(1)}) custom-call(s32[3]{0:T(128)S(1)} %copy-done, bf16[128,2432]{1,0:T(8,128)(2,1)S(1)} %pad_maximum_fusion.data.home_data, f32[8,128]{1,0:T(8,128)S(1)} %copy-done.3, bf16[512,768]{1,0:T(8,128)(2,1)S(1)} %bitcast.38, bf16[512,768]{1,0:T(8,128)(2,1)} %collective-permute-done.refs_1_, ...), custom_call_target="tpu_custom_call" | custom-call | flops 1207959552 | bytes 6291456 | tf_op jit(solution)/shard_map/home/pallas_call | solution.py:155
  51.5 5.0 %all-to-all-done.3 = bf16[8,16,2432]{2,1,0:T(8,128)(2,1)S(1)} async-done(((bf16[8,16,2432]{2,1,0:T(8,128)(2,1)}), bf16[8,16,2432]{2,1,0:T(8,128)(2,1)S(1)}, u32[]{:S(2)}, u32[]{:S(2)}) %all-to-all-start.3) | async-done | bytes 622624 | tf_op jit(solution)/shard_map/all_to_all | solution.py:116
  56.5 4.2 %all-to-all-start.1 = ((bf16[8,24,2048]{2,1,0:T(8,128)(2,1)}), bf16[8,24,2048]{2,1,0:T(8,128)(2,1)}, u32[]{:S(2)}, u32[]{:S(2)}) async-start(bf16[8,24,2048]{2,1,0:T(8,128)(2,1)} %bitcast.12), calls=%async_computation.1 | async-start | bytes 1572864 | tf_op jit(solution)/shard_map/all_to_all | solution.py:116
  60.8 4.3 %replica.1 = (bf16[192,2048]{1,0:T(8,128)(2,1)}, bf16[128,768]{1,0:T(8,128)(2,1)S(1)}) custom-call(s32[3]{0:T(128)S(1)} %copy-done.1, bf16[128,2432]{1,0:T(8,128)(2,1)S(1)} %bitcast.34, f32[8,128]{1,0:T(8,128)S(1)} %copy-done.4, bf16[512,768]{1,0:T(8,128)(2,1)S(1)} %bitcast.39, bf16[512,768]{1,0:T(8,128)(2,1)} %collective-permute-done.refs_1_, ...), custom_call_target="tpu_custom_call" | custom-call | flops 1207959552 | bytes 6291456 | tf_op jit(solution)/shard_map/replica/pallas_call | solution.py:155
  65.1 2.7 %weight_grad.1 = (bf16[2,512,768]{2,1,0:T(8,128)(2,1)S(1)}, bf16[2,512,768]{2,1,0:T(8,128)(2,1)}) custom-call(s32[3]{0:T(128)S(1)} %copy-done.1, bf16[128,2432]{1,0:T(8,128)(2,1)S(1)} %pad_maximum_fusion.data.home_data, bf16[128,2432]{1,0:T(8,128)(2,1)S(1)} %bitcast.35, bf16[128,768]{1,0:T(8,128)(2,1)S(1)} %get-tuple-element.16.home_grads, ...), custom_call_target="tpu_custom_call" | custom-call | flops 805306368 | bytes 6291456 | tf_op jit(solution)/shard_map/weight_grad/pallas_call | solution.py:180
  67.8 12.3 %all-to-all-done.1 = bf16[8,24,2048]{2,1,0:T(8,128)(2,1)} async-done(((bf16[8,24,2048]{2,1,0:T(8,128)(2,1)}), bf16[8,24,2048]{2,1,0:T(8,128)(2,1)}, u32[]{:S(2)}, u32[]{:S(2)}) %all-to-all-start.1) | async-done | bytes 786464 | tf_op jit(solution)/shard_map/all_to_all | solution.py:116
  80.1 4.2 %all-to-all-start.4 = ((bf16[8,24,2048]{2,1,0:T(8,128)(2,1)}), bf16[8,24,2048]{2,1,0:T(8,128)(2,1)}, u32[]{:S(2)}, u32[]{:S(2)}) async-start(bf16[8,24,2048]{2,1,0:T(8,128)(2,1)} %bitcast.17), calls=%async_computation.4 | async-start | bytes 1572864 | tf_op jit(solution)/shard_map/all_to_all | solution.py:116
  84.7 1.6 %copy-done.5 = f32[2,512,768]{2,1,0:T(8,128)} copy-done((f32[2,512,768]{2,1,0:T(8,128)}, f32[2,512,768]{2,1,0:T(8,128)S(1)}, u32[]{:S(2)}) %copy-start.5) | copy-done | bytes 3145752
  86.3 1.0 slice.23
  87.3 1.5 %collective-permute-start.4 = (bf16[1,512,768]{2,1,0:T(8,128)(2,1)}, bf16[1,512,768]{2,1,0:T(8,128)(2,1)}, u32[]{:S(2)}, u32[]{:S(2)}) collective-permute-start(bf16[1,512,768]{2,1,0:T(8,128)(2,1)} %slice.23), channel_id=1, source_target_pairs={{0,2},{1,3},{2,0},{3,1},{4,6},{5,7},{6,4},{7,5},{8,10},{9,11},{10,... | collective-permute-start | bytes 2359304 | tf_op jit(solution)/shard_map/ppermute | solution.py:113
  88.9 2.6 %fusion.2 = f32[128,2048]{1,0:T(8,128)} fusion(bf16[192,2048]{1,0:T(8,128)(2,1)} %bitcast.13, s32[192]{0:T(256)S(1)} %eq.54), kind=kOutput, calls=%fused_computation.11 | convolution fusion | flops 100687872 | bytes 1835776 | tf_op jit(solution)/shard_map/dot_general | solution.py:173
  91.5 12.6 %all-to-all-done.4 = bf16[8,24,2048]{2,1,0:T(8,128)(2,1)} async-done(((bf16[8,24,2048]{2,1,0:T(8,128)(2,1)}), bf16[8,24,2048]{2,1,0:T(8,128)(2,1)}, u32[]{:S(2)}, u32[]{:S(2)}) %all-to-all-start.4) | async-done | bytes 786464 | tf_op jit(solution)/shard_map/all_to_all | solution.py:116
  104.1 2.6 %fusion.1 = bf16[1,128,2048]{2,1,0:T(8,128)(2,1)} fusion(f32[128,2048]{1,0:T(8,128)} %fusion.2, bf16[192,2048]{1,0:T(8,128)(2,1)} %bitcast.18, s32[192]{0:T(256)S(1)} %eq.58), kind=kOutput, calls=%fused_computation.4 | convolution fusion | flops 101212160 | bytes 2360064 | tf_op jit(solution)/shard_map/dot_general | solution.py:173
  106.7 2.4 %slice_add_fusion = f32[1,512,768]{2,1,0:T(8,128)} fusion(f32[2,512,768]{2,1,0:T(8,128)S(1)} %copy-done.6, bf16[1,512,768]{2,1,0:T(8,128)(2,1)} %collective-permute-done.4), kind=kLoop, calls=%fused_computation.6 | loop fusion | flops 786432 | bytes 3932160 | tf_op jit(solution)/shard_map/add | solution.py:194
  (52 shorter events, 5.7 us)
Async XLA Ops:
  0.6 9.4 %copy-start.2 = (bf16[1,512,768]{2,1,0:T(8,128)(2,1)S(1)}, bf16[1,512,768]{2,1,0:T(8,128)(2,1)}, u32[]{:S(2)}) copy-start(bf16[1,512,768]{2,1,0:T(8,128)(2,1)} %param.15) | copy-start | bytes 2359300
  0.6 11.0 %copy-start.15 = (bf16[1,128]{1,0:T(2,128)(2,1)S(1)}, bf16[1,128]{1,0:T(2,128)(2,1)}, u32[]{:S(2)}) copy-start(bf16[1,128]{1,0:T(2,128)(2,1)} %param.10) | copy-start | bytes 772
  0.7 11.0 %copy-start.11 = (s32[1,1,2]{2,1,0:T(1,128)S(1)}, s32[1,1,2]{2,1,0:T(1,128)}, u32[]{:S(2)}) copy-start(s32[1,1,2]{2,1,0:T(1,128)} %param.11) | copy-start | bytes 28
  0.7 12.8 %copy-start.12 = (s32[1,128]{1,0:T(1,128)S(1)}, s32[1,128]{1,0:T(1,128)}, u32[]{:S(2)}) copy-start(s32[1,128]{1,0:T(1,128)} %param.13) | copy-start | bytes 1540
  0.7 12.8 %copy-start.13 = (s32[1,128,1]{1,2,0:T(1,128)S(1)}, s32[1,128,1]{1,2,0:T(1,128)}, u32[]{:S(2)}) copy-start(s32[1,128,1]{1,2,0:T(1,128)} %param.12) | copy-start | bytes 1540
  0.7 13.4 %copy-start.14 = (s32[8]{0:T(128)S(1)}, s32[8]{0:T(128)}, u32[]{:S(2)}) copy-start(s32[8]{0:T(128)} %param.14) | copy-start | bytes 100
  2.7 23.9 %all-to-all-start.2 = ((bf16[8,16,2432]{2,1,0:T(8,128)(2,1)}), bf16[8,16,2432]{2,1,0:T(8,128)(2,1)S(1)}, u32[]{:S(2)}, u32[]{:S(2)}) async-start(bf16[8,16,2432]{2,1,0:T(8,128)(2,1)} %pad_maximum_fusion.1), calls=%async_computation.2 | async-start | bytes 1245184 | tf_op jit(solution)/shard_map/all_to_all | solution.py:116
  10.0 33.4 %copy-start.7 = (bf16[1,128,2048]{2,1,0:T(8,128)(2,1)S(1)}, bf16[1,128,2048]{2,1,0:T(8,128)(2,1)}, u32[]{:S(2)}) copy-start(bf16[1,128,2048]{2,1,0:T(8,128)(2,1)} %param.8) | copy-start | bytes 1572868
  10.0 33.4 %copy-start.8 = (bf16[1,128,384]{2,1,0:T(8,128)(2,1)S(1)}, bf16[1,128,384]{2,1,0:T(8,128)(2,1)}, u32[]{:S(2)}) copy-start(bf16[1,128,384]{2,1,0:T(8,128)(2,1)} %param.9) | copy-start | bytes 294916
  10.1 31.0 %collective-permute-start.1 = (bf16[512,768]{1,0:T(8,128)(2,1)S(1)}, bf16[512,768]{1,0:T(8,128)(2,1)S(1)}, u32[]{:S(2)}, u32[]{:S(2)}) collective-permute-start(bf16[512,768]{1,0:T(8,128)(2,1)S(1)} %bitcast.36), channel_id=1, source_target_pairs={{0,2},{1,3},{2,0},{3,1},{4,6},{5,7},{6,4},{7,5},{8,10},{9,11},{10,... | collective-permute-start | bytes 2359304 | tf_op jit(solution)/shard_map/ppermute | solution.py:113
  27.2 10.2 %all-to-all-start = ((f32[8,1,256]{2,1,0:T(1,128)}), f32[8,1,256]{2,1,0:T(1,128)S(1)}, u32[]{:S(2)}, u32[]{:S(2)}) async-start(f32[8,1,256]{2,1,0:T(1,128)} %broadcast_in_dim.45), calls=%async_computation | async-start | bytes 16384 | tf_op jit(solution)/shard_map/all_to_all | solution.py:116
  37.4 19.1 %all-to-all-start.3 = ((bf16[8,16,2432]{2,1,0:T(8,128)(2,1)}), bf16[8,16,2432]{2,1,0:T(8,128)(2,1)S(1)}, u32[]{:S(2)}, u32[]{:S(2)}) async-start(bf16[8,16,2432]{2,1,0:T(8,128)(2,1)} %gather_fusion), calls=%async_computation.3 | async-start | bytes 1245184 | tf_op jit(solution)/shard_map/all_to_all | solution.py:116
  40.9 4.9 %collective-permute-start = (bf16[512,768]{1,0:T(8,128)(2,1)S(1)}, bf16[512,768]{1,0:T(8,128)(2,1)}, u32[]{:S(2)}, u32[]{:S(2)}) collective-permute-start(bf16[512,768]{1,0:T(8,128)(2,1)S(1)} %bitcast.37), channel_id=1, source_target_pairs={{0,1},{1,0},{2,3},{3,2},{4,5},{5,4},{6,7},{7,6},{8,9},{9,8},{10,11... | collective-permute-start | bytes 2359304 | tf_op jit(solution)/shard_map/ppermute | solution.py:113
  41.0 4.8 %collective-permute-start.2 = (bf16[512,768]{1,0:T(8,128)(2,1)S(1)}, bf16[512,768]{1,0:T(8,128)(2,1)}, u32[]{:S(2)}, u32[]{:S(2)}) collective-permute-start(bf16[512,768]{1,0:T(8,128)(2,1)S(1)} %collective-permute-done.1.refs_2_), channel_id=1, source_target_pairs={{0,1},{1,0},{2,3},{3,2},{4,5},{5,4},{6,7},{7,6},{8,9},{9,8},{10,11... | collective-permute-start | bytes 2359304 | tf_op jit(solution)/shard_map/ppermute | solution.py:113
  51.5 9.3 %copy-start.1 = (s32[3]{0:T(128)S(1)}, s32[3]{0:T(128)}, u32[]{:S(2)}) copy-start(s32[3]{0:T(128)} %pad_add_fusion.ids) | copy-start | bytes 40
  51.5 9.3 %copy-start.4 = (f32[8,128]{1,0:T(8,128)S(1)}, f32[8,128]{1,0:T(8,128)}, u32[]{:S(2)}) copy-start(f32[8,128]{1,0:T(8,128)} %get-tuple-element.12.ctl) | copy-start | bytes 12292
  56.5 23.6 %all-to-all-start.1 = ((bf16[8,24,2048]{2,1,0:T(8,128)(2,1)}), bf16[8,24,2048]{2,1,0:T(8,128)(2,1)}, u32[]{:S(2)}, u32[]{:S(2)}) async-start(bf16[8,24,2048]{2,1,0:T(8,128)(2,1)} %bitcast.12), calls=%async_computation.1 | async-start | bytes 1572864 | tf_op jit(solution)/shard_map/all_to_all | solution.py:116
  67.8 16.5 %collective-permute-start.3 = (bf16[2,512,768]{2,1,0:T(8,128)(2,1)}, bf16[2,512,768]{2,1,0:T(8,128)(2,1)S(1)}, u32[]{:S(2)}, u32[]{:S(2)}) collective-permute-start(bf16[2,512,768]{2,1,0:T(8,128)(2,1)} %get-tuple-element.19), channel_id=1, source_target_pairs={{0,1},{1,0},{2,3},{3,2},{4,5},{5,4},{6,7},{7,6},{8,9},{9,8},{10,11... | collective-permute-start | bytes 4718600 | tf_op jit(solution)/shard_map/ppermute | solution.py:113
  80.1 24.0 %all-to-all-start.4 = ((bf16[8,24,2048]{2,1,0:T(8,128)(2,1)}), bf16[8,24,2048]{2,1,0:T(8,128)(2,1)}, u32[]{:S(2)}, u32[]{:S(2)}) async-start(bf16[8,24,2048]{2,1,0:T(8,128)(2,1)} %bitcast.17), calls=%async_computation.4 | async-start | bytes 1572864 | tf_op jit(solution)/shard_map/all_to_all | solution.py:116
  84.7 1.6 %copy-start.5 = (f32[2,512,768]{2,1,0:T(8,128)}, f32[2,512,768]{2,1,0:T(8,128)S(1)}, u32[]{:S(2)}) copy-start(f32[2,512,768]{2,1,0:T(8,128)S(1)} %convert_add_fusion) | copy-start | bytes 9437188
  86.3 2.5 %copy-start.10 = (s32[8,24]{1,0:T(8,128)S(1)}, s32[8,24]{1,0:T(8,128)}, u32[]{:S(2)}) copy-start(s32[8,24]{1,0:T(8,128)} %get-tuple-element.11) | copy-start | bytes 2308
  86.3 2.5 %copy-start.9 = (s32[8,24]{1,0:T(8,128)S(1)}, s32[8,24]{1,0:T(8,128)}, u32[]{:S(2)}) copy-start(s32[8,24]{1,0:T(8,128)} %get-tuple-element.14) | copy-start | bytes 2308
  87.3 19.4 %collective-permute-start.4 = (bf16[1,512,768]{2,1,0:T(8,128)(2,1)}, bf16[1,512,768]{2,1,0:T(8,128)(2,1)}, u32[]{:S(2)}, u32[]{:S(2)}) collective-permute-start(bf16[1,512,768]{2,1,0:T(8,128)(2,1)} %slice.23), channel_id=1, source_target_pairs={{0,2},{1,3},{2,0},{3,1},{4,6},{5,7},{6,4},{7,5},{8,10},{9,11},{10,... | collective-permute-start | bytes 2359304 | tf_op jit(solution)/shard_map/ppermute | solution.py:113
  88.9 17.7 %copy-start.6 = (f32[2,512,768]{2,1,0:T(8,128)S(1)}, f32[2,512,768]{2,1,0:T(8,128)}, u32[]{:S(2)}) copy-start(f32[2,512,768]{2,1,0:T(8,128)} %copy-done.5) | copy-start | bytes 9437188
  (2 other events, 1.3 us)
